TPU v7x, 16 devices: a whole 2x2x2 slice. The times are simulated.
16 devices in a mesh: dp: 4 (over z, y), sh: 4 (over x, core).
Axes of the slice: x: 2, y: 2, z: 2, core: 2. Of those that a mesh axis runs over, the one named last changes fastest.
Arguments:
- k_prefill: bfloat16 [16, 7168, 8, 256], P('dp', None, 'sh'), parts along dimension 0
- v_prefill: bfloat16 [16, 7168, 8, 256], P('dp', None, 'sh'), parts along dimension 0
- lengths: int32 [16], P('dp'), parts along dimension 0
- residual: bfloat16 [16, 3584], P(('dp', 'sh')), parts along dimension 0
- norm_gain: bfloat16 [3584], replicated
- w_query: bfloat16 [3584, 4096], replicated
- w_key: bfloat16 [3584, 2048], replicated
- w_value: bfloat16 [3584, 2048], replicated
- w_out: bfloat16 [4096, 3584], replicated
Outputs:
- output 1: bfloat16 [16, 3584], P(('dp', 'sh')), parts along dimension 0
- output 2: bfloat16 [16, 4096, 8, 256], P(('dp', 'sh')), parts along dimension 0
- output 3: bfloat16 [16, 4096, 8, 256], P(('dp', 'sh')), parts along dimension 0
There are 4 independent parts. A program takes and returns all parts, laid end to end along the dimension named above; an argument that names none is the same for every part.
All inputs are finite; a program needn't handle non-finite values.
Results may differ from a plain program's by a relative error of at most 0.00415.
Values are sent between devices in bfloat16 or wider.
A program may use at most 1 GiB of HBM per device.

v0:
```python
import jax
import jax.numpy as jnp
from jax import lax
from jax.sharding import PartitionSpec as P

WINDOW = 4096
THETA = 10000.0
EPS = 1e-5


def rolling_rows(prefill, lengths):
    def one_row(row_vals, row_len):
        first_pos = jnp.maximum(row_len - WINDOW, 0)
        win_vals = lax.dynamic_slice_in_dim(row_vals, first_pos, WINDOW, axis=0)
        positions = first_pos + jnp.arange(WINDOW, dtype=jnp.int32)
        win_vals = jnp.where((positions < row_len)[:, None, None], win_vals, jnp.zeros((), win_vals.dtype))
        doubled = jnp.concatenate([win_vals, win_vals], axis=0)
        return lax.dynamic_slice_in_dim(doubled, WINDOW - first_pos % WINDOW, WINDOW, axis=0)
    return jax.vmap(one_row)(prefill, lengths)


def rotate(heads, positions):
    head_dim = heads.shape[-1]
    half_dim = head_dim // 2
    inv_freq = THETA ** (-2.0 * jnp.arange(half_dim, dtype=jnp.float32) / head_dim)
    angles = positions.astype(jnp.float32).reshape(positions.shape + (1,) * (heads.ndim - 1)) * inv_freq
    cos_part = jnp.cos(angles)
    sin_part = jnp.sin(angles)
    first_half = heads[..., :half_dim].astype(jnp.float32)
    second_half = heads[..., half_dim:].astype(jnp.float32)
    return jnp.concatenate([first_half * cos_part - second_half * sin_part, second_half * cos_part + first_half * sin_part], axis=-1).astype(jnp.bfloat16)


def decode_rows(residual, lengths, k_cache, v_cache, norm_gain, w_query, w_key, w_value, w_out):
    num_rows = residual.shape[0]
    kv_heads = k_cache.shape[2]
    head_dim = k_cache.shape[3]
    q_group = w_query.shape[1] // (kv_heads * head_dim)
    resid_f32 = residual.astype(jnp.float32)
    inv_rms = lax.rsqrt(jnp.mean(resid_f32 * resid_f32, axis=-1, keepdims=True) + EPS)
    normed = (resid_f32 * inv_rms * norm_gain.astype(jnp.float32)).astype(jnp.bfloat16)
    q_heads = jnp.dot(normed, w_query, preferred_element_type=jnp.float32).astype(jnp.bfloat16).reshape(num_rows, kv_heads, q_group, head_dim)
    k_new = jnp.dot(normed, w_key, preferred_element_type=jnp.float32).astype(jnp.bfloat16).reshape(num_rows, kv_heads, head_dim)
    v_new = jnp.dot(normed, w_value, preferred_element_type=jnp.float32).astype(jnp.bfloat16).reshape(num_rows, kv_heads, head_dim)
    q_heads = rotate(q_heads, lengths)
    k_new = rotate(k_new, lengths)
    slot_ids = jnp.arange(WINDOW, dtype=jnp.int32)
    new_slot = (slot_ids[None, :] == (lengths % WINDOW)[:, None])[:, :, None, None]
    k_cache = jnp.where(new_slot, k_new[:, None], k_cache)
    v_cache = jnp.where(new_slot, v_new[:, None], v_cache)
    live_slot = (lengths[:, None] - jnp.remainder(lengths[:, None] - slot_ids[None, :], WINDOW)) >= 0
    scores = jnp.einsum('rkgd,rwkd->rkgw', q_heads, k_cache, preferred_element_type=jnp.float32) / head_dim ** 0.5
    scores = jnp.where(live_slot[:, None, None, :], scores, -jnp.inf)
    exp_scores = jnp.exp(scores - jnp.max(scores, axis=-1, keepdims=True))
    weights = (exp_scores / jnp.sum(exp_scores, axis=-1, keepdims=True)).astype(jnp.bfloat16)
    attn_out = jnp.einsum('rkgw,rwkd->rkgd', weights, v_cache, preferred_element_type=jnp.float32).astype(jnp.bfloat16).reshape(num_rows, kv_heads * q_group * head_dim)
    resid_out = (resid_f32 + jnp.dot(attn_out, w_out, preferred_element_type=jnp.float32)).astype(jnp.bfloat16)
    return resid_out, k_cache, v_cache


def solution(mesh):
    head_spec = P('dp', None, 'sh', None)
    row_spec = P(('dp', 'sh'))
    full_spec = P(None, None)

    def per_device(k_prefill, v_prefill, lengths, residual, norm_gain, w_query, w_key, w_value, w_out):
        num_rows = residual.shape[0]
        my_lengths = lax.dynamic_slice_in_dim(lengths, lax.axis_index('sh') * num_rows, num_rows)
        k_rows = lax.all_to_all(k_prefill, 'sh', 0, 2, tiled=True)
        v_rows = lax.all_to_all(v_prefill, 'sh', 0, 2, tiled=True)
        k_cache = rolling_rows(k_rows, my_lengths)
        v_cache = rolling_rows(v_rows, my_lengths)
        return decode_rows(residual, my_lengths, k_cache, v_cache, norm_gain, w_query, w_key, w_value, w_out)
    return jax.shard_map(per_device, mesh=mesh, in_specs=(head_spec, head_spec, P('dp'), P(('dp', 'sh'), None), P(None), full_spec, full_spec, full_spec, full_spec), out_specs=(P(('dp', 'sh'), None), row_spec, row_spec), check_vma=False)
```

profile of v0, /device:TPU:0, one launch (start us, length us, event | category | flops | bytes accessed | tf_op | source)
XLA Modules:
  0.0 836.3 jit_solution(10061690368246312598)
XLA Ops:
  0.6 334.9 %all_to_all.36 = bf16[4,7168,2,256]{3,2,1,0:T(2,128)(2,1)} all-to-all(bf16[4,7168,2,256]{3,2,1,0:T(2,128)(2,1)} %param.9), channel_id=1, replica_groups=mesh['dp'=4,'sh'=4] {'sh'}, dimensions={0} | all-to-all | bytes 58720256 | tf_op jit(solution)/shard_map/all_to_all | solution.py:69
  335.5 0.0 copy-start.2
  335.5 0.0 copy-start.1
  335.5 0.0 copy-start
  335.5 9.2 %all-to-all-start.1 = ((bf16[4,7168,2,256]{3,2,1,0:T(2,128)(2,1)}), bf16[4,7168,2,256]{3,2,1,0:T(2,128)(2,1)}, u32[]{:S(2)}, u32[]{:S(2)}) async-start(bf16[4,7168,2,256]{3,2,1,0:T(2,128)(2,1)} %param.10), calls=%async_computation.1 | async-start | bytes 58720256 | tf_op jit(solution)/shard_map/all_to_all | solution.py:70
  344.8 0.0 copy-done.2
  344.8 0.6 dynamic_slice.3
  348.6 0.0 copy-done.1
  348.6 0.0 copy-done
  348.6 0.6 multiply_reduce_fusion
  350.0 7.2 fusion.28
  357.2 7.2 fusion.26
  364.4 11.4 %fusion.30 = f32[1,4096]{1,0:T(1,128)S(1)} fusion(bf16[3584,4096]{1,0:T(8,128)(2,1)} %param.14, f32[3584]{0:T(1024)S(1)} %broadcast_in_dim.110, bf16[1,3584]{1,0:T(2,128)(2,1)S(1)} %copy-done, f32[]{:T(128)S(6)} %rsqrt.4), kind=kOutput, calls=%fused_computation.41 | convolution fusion | flops 29374464 | bytes 29398020 | tf_op jit(solution)/shard_map/dot_general | solution.py:42
  375.8 0.1 fusion.48
  375.9 0.7 fusion.22
  376.6 23.8 %copy.14 = bf16[1,7168,4,2,256]{4,3,2,1,0:T(2,128)(2,1)} copy(bf16[1,7168,4,2,256]{4,3,1,2,0:T(2,128)(2,1)} %bitcast.39) | data formatting | bytes 58720256 | tf_op jit(solution)/shard_map/all_to_all | solution.py:69
  400.4 42.6 %all_to_all.29 = bf16[1,7168,8,256]{3,2,1,0:T(8,128)(2,1)} reshape(bf16[1,7168,4,2,256]{4,3,2,1,0:T(2,128)(2,1)} %copy.14) | data formatting | bytes 58720256 | tf_op jit(solution)/shard_map/all_to_all | solution.py:69
  443.0 219.3 %all-to-all-done.1 = bf16[4,7168,2,256]{3,2,1,0:T(2,128)(2,1)} async-done(((bf16[4,7168,2,256]{3,2,1,0:T(2,128)(2,1)}), bf16[4,7168,2,256]{3,2,1,0:T(2,128)(2,1)}, u32[]{:S(2)}, u32[]{:S(2)}) %all-to-all-start.1) | async-done | bytes 29360160 | tf_op jit(solution)/shard_map/all_to_all | solution.py:70
  662.3 23.8 %copy.16 = bf16[1,7168,4,2,256]{4,3,2,1,0:T(2,128)(2,1)} copy(bf16[1,7168,4,2,256]{4,3,1,2,0:T(2,128)(2,1)} %bitcast.16) | data formatting | bytes 58720256 | tf_op jit(solution)/shard_map/all_to_all | solution.py:70
  686.1 42.5 %all_to_all.33 = bf16[1,7168,8,256]{3,2,1,0:T(8,128)(2,1)} reshape(bf16[1,7168,4,2,256]{4,3,2,1,0:T(2,128)(2,1)} %copy.16) | data formatting | bytes 58720256 | tf_op jit(solution)/shard_map/all_to_all | solution.py:70
  728.6 23.0 %dynamic-slice_select_fusion.1 = (bf16[1,4096,8,256]{3,2,1,0:T(8,128)(2,1)}, bf16[1,4096,8,256]{3,2,1,0:T(8,128)(2,1)}) fusion(bf16[1,7168,8,256]{3,2,1,0:T(8,128)(2,1)} %all_to_all.29, s32[]{:T(128)} %bitcast.9, pred[4096]{0:T(1024)(128)(4,1)S(1)} %get-tuple-element.62, bf16[1,7168,8,256]{3,2,1,0:T(8,128)(2,1)} %all_to_all.33), kind=kLoop, calls=%fused_computation.14 | loop fusion | flops 16777216 | bytes 67112960 | tf_op jit(solution)/shard_map/vmap(jit(_where))/select_n | solution.py:16
  751.6 26.0 %bitcast_select_fusion.1 = (bf16[4096,8,256]{2,1,0:T(8,128)(2,1)}, bf16[4096,8,256]{2,1,0:T(8,128)(2,1)}) fusion(pred[4096]{0:T(1024)(128)(4,1)S(1)} %iota_compare_fusion, bf16[8,256]{1,0:T(8,128)(2,1)S(1)} %pad_maximum_fusion, s32[]{:T(128)} %bitcast.12, bf16[1,4096,8,256]{3,2,1,0:T(8,128)(2,1)} %get-tuple-element.55, ...), kind=kLoop, calls=%fused_computation.8 | loop fusion | flops 33554432 | bytes 67121152 | tf_op jit(solution)/shard_map/jit(_where)/select_n | solution.py:49
  777.6 25.9 %broadcast_select_fusion = (bf16[1,4096,8,256]{3,2,1,0:T(8,128)(2,1)}, bf16[1,4096,8,256]{3,2,1,0:T(8,128)(2,1)}) fusion(pred[4096]{0:T(1024)(128)(4,1)S(1)} %iota_compare_fusion, bf16[8,256]{1,0:T(8,128)(2,1)S(1)} %broadcast_in_dim.105, s32[]{:T(128)} %bitcast.12, bf16[1,4096,8,256]{3,2,1,0:T(8,128)(2,1)} %get-tuple-element.56, ...), kind=kLoop, calls=%fused_computation.15 | loop fusion | flops 33554432 | bytes 67121152 | tf_op jit(solution)/shard_map/jit(_where)/select_n | solution.py:50
  803.5 10.4 %fusion.12 = f32[8,2,4096]{2,1,0:T(2,128)S(1)} fusion(bf16[4096,8,256]{2,1,0:T(8,128)(2,1)} %get-tuple-element.53, pred[4096]{0:T(1024)(128)(4,1)S(1)} %get-tuple-element.61, bf16[8,2,128]{2,1,0:T(2,128)(2,1)S(1)} %get-tuple-element.48, bf16[8,2,128]{2,1,0:T(2,128)(2,1)S(1)} %get-tuple-element.47), kind=kOutput, calls=%fused_computation.20 | convolution fusion | flops 33701888 | bytes 17051648 | tf_op jit(solution)/shard_map/rkgd,rwkd->rkgw/dot_general | solution.py:52
  813.9 0.4 fusion.51
  814.3 10.1 %fusion.16 = bf16[8,2,256]{2,1,0:T(2,128)(2,1)S(1)} fusion(bf16[4096,8,256]{2,1,0:T(8,128)(2,1)} %get-tuple-element.54, f32[8,2,4096]{2,1,0:T(2,128)S(1)} %get-tuple-element.58, f32[8,2]{1,0:T(8,128)S(1)} %get-tuple-element.57), kind=kOutput, calls=%fused_computation.23 | convolution fusion | flops 33689600 | bytes 17047616 | tf_op jit(solution)/shard_map/rkgw,rwkd->rkgd/dot_general | solution.py:56
  824.4 12.0 %fusion.15 = bf16[1,3584]{1,0:T(2,128)(2,1)} fusion(bf16[4096,1]{0,1:T(2,128)(2,1)S(1)} %reshape.373, bf16[4096,3584]{1,0:T(8,128)(2,1)} %param.17, bf16[1,3584]{1,0:T(2,128)(2,1)S(1)} %copy-done), kind=kOutput, calls=%fused_computation.22 | convolution fusion | flops 29370880 | bytes 29382656 | tf_op jit(solution)/shard_map/dot_general | solution.py:57
  (12 shorter events, 0.1 us)
Async XLA Ops:
  335.5 9.3 %copy-start.2 = (s32[4]{0:T(128)S(1)}, s32[4]{0:T(128)}, u32[]{:S(2)}) copy-start(s32[4]{0:T(128)} %param.11) | copy-start | bytes 52
  335.5 13.1 %copy-start.1 = (bf16[3584]{0:T(1024)(128)(2,1)S(1)}, bf16[3584]{0:T(1024)(128)(2,1)}, u32[]{:S(2)}) copy-start(bf16[3584]{0:T(1024)(128)(2,1)} %param.13) | copy-start | bytes 21508
  335.5 13.1 %copy-start = (bf16[1,3584]{1,0:T(2,128)(2,1)S(1)}, bf16[1,3584]{1,0:T(2,128)(2,1)}, u32[]{:S(2)}) copy-start(bf16[1,3584]{1,0:T(2,128)(2,1)} %param.12) | copy-start | bytes 21508
  335.5 326.8 %all-to-all-start.1 = ((bf16[4,7168,2,256]{3,2,1,0:T(2,128)(2,1)}), bf16[4,7168,2,256]{3,2,1,0:T(2,128)(2,1)}, u32[]{:S(2)}, u32[]{:S(2)}) async-start(bf16[4,7168,2,256]{3,2,1,0:T(2,128)(2,1)} %param.10), calls=%async_computation.1 | async-start | bytes 58720256 | tf_op jit(solution)/shard_map/all_to_all | solution.py:70
where the time goes:
time: 839 us; the launch traced here: 836 us
  blocking collectives  335 us (40%)
  waiting for transfers between devices  219 us (26%)
  local copies, waits for them, and re-layouts  133 us (16%)
  other arithmetic  76.7 us (9%)
  matrix products  58.2 us (7%)
  starting transfers between devices  9.24 us (1%)
    all_to_all x1, blocking collectives, per_device(): k_rows = lax.all_to_all(k_prefill, 'sh', 0, 2, tiled=True)  335 us
    all_to_all x1, waiting for transfers between devices, per_device(): v_rows = lax.all_to_all(v_prefill, 'sh', 0, 2, tiled=True)  219 us
    all_to_all x2, local copies, waits for them, and re-layouts, per_device(): k_rows = lax.all_to_all(k_prefill, 'sh', 0, 2, tiled=True)  66.4 us
    all_to_all x2, local copies, waits for them, and re-layouts, per_device(): v_rows = lax.all_to_all(v_prefill, 'sh', 0, 2, tiled=True)  66.3 us
    select_n x1, other arithmetic, decode_rows(): k_cache = jnp.where(new_slot, k_new[:, None], k_cache)  26 us
    select_n x1, other arithmetic, decode_rows(): v_cache = jnp.where(new_slot, v_new[:, None], v_cache)  25.9 us
    select_n x1, other arithmetic, one_row(): jnp.where((positions < row_len)[:, None, None], win_vals, jnp.zeros((), w...  23 us
  transfers between devices with their start and end apart: 1, of which 1 were waited for; matrix products, arithmetic and copies ran while one was open for 6% of the time, Pallas kernels for 0%

commit v1 on v0

v1 whole, which is shorter than its diff:
```python
import functools

import jax
import jax.numpy as jnp
from jax import lax
from jax.experimental import pallas as pl
from jax.experimental.pallas import tpu as pltpu
from jax.sharding import PartitionSpec as P


WINDOW = 4096
THETA = 10000.0
EPS = 1e-5
LANES = 128
BLOCK = 256
DEPTH = 4
VMEM_BYTES = 67043328
K_CHUNKS = (512, 1536, 2048)
V_CHUNKS = (2048, 1536, 512)


def build_kernel(pieces, scal_ref, src_ref, _, *refs):
    outs = refs[:len(pieces)]
    buf, other, zeros, in_sem, other_sem, out_sem = refs[len(pieces):]
    me = scal_ref[4]
    last = src_ref.shape[1] - BLOCK
    zeros[...] = jnp.zeros_like(zeros)

    for (j, c0, size), out in zip(pieces, outs):
        row = me ^ j
        length = scal_ref[row]
        wrapped = jnp.maximum(length - WINDOW, 0)
        filled = jnp.minimum(length, WINDOW)
        count = size // BLOCK

        def start_in(i):
            base = c0 + i * BLOCK
            slot = lax.rem(i, DEPTH)
            whole_wrapped = base + BLOCK <= wrapped
            first = jnp.where(whole_wrapped, jnp.minimum(base + WINDOW, last), base)

            @pl.when(base < filled)
            def _():
                pltpu.make_async_copy(src_ref.at[row, pl.ds(first, BLOCK)], buf.at[slot], in_sem.at[slot]).start()

            @pl.when((base < wrapped) & (base + BLOCK > wrapped))
            def _():
                pltpu.make_async_copy(src_ref.at[row, pl.ds(jnp.minimum(base + WINDOW, last), BLOCK)], other, other_sem).start()

        def out_copy(i):
            slot = lax.rem(i, DEPTH)
            return pltpu.make_async_copy(buf.at[slot], out.at[pl.ds(i * BLOCK, BLOCK)], out_sem.at[slot])

        def finish(i):
            base = c0 + i * BLOCK
            slot = lax.rem(i, DEPTH)

            @pl.when(base < filled)
            def _():
                pltpu.make_async_copy(src_ref.at[row, pl.ds(0, BLOCK)], buf.at[slot], in_sem.at[slot]).wait()

                @pl.when((base < wrapped) & (base + BLOCK > wrapped))
                def _():
                    pltpu.make_async_copy(src_ref.at[row, pl.ds(0, BLOCK)], other, other_sem).wait()

                    @pl.loop(0, wrapped - base)
                    def _(s):
                        buf[slot, s] = other[s]

                @pl.when(base + BLOCK > filled)
                def _():
                    @pl.loop(filled - base, BLOCK)
                    def _(s):
                        buf[slot, s] = zeros[0]

                out_copy(i).start()

            @pl.when(base >= filled)
            def _():
                pltpu.make_async_copy(zeros, out.at[pl.ds(i * BLOCK, BLOCK)], out_sem.at[slot]).start()

        for i in range(min(DEPTH - 1, count)):
            start_in(i)

        @pl.loop(0, count)
        def _(i):
            finish(i)
            ahead = i + DEPTH - 1

            @pl.when(ahead < count)
            def _():
                @pl.when(i >= 1)
                def _():
                    out_copy(i - 1).wait()

                start_in(ahead)

        for i in range(max(count - DEPTH, 0), count):
            out_copy(i).wait()


def build(scal, src, pieces, after):
    tile = src.shape[2:]
    return pl.pallas_call(
        functools.partial(build_kernel, pieces),
        out_shape=[jax.ShapeDtypeStruct((size,) + tile, src.dtype) for _, _, size in pieces],
        in_specs=[pl.BlockSpec(memory_space=pltpu.SMEM), pl.BlockSpec(memory_space=pltpu.HBM), pl.BlockSpec(memory_space=pl.ANY)],
        out_specs=[pl.BlockSpec(memory_space=pltpu.HBM)] * len(pieces),
        scratch_shapes=[
            pltpu.VMEM((DEPTH, BLOCK) + tile, src.dtype),
            pltpu.VMEM((BLOCK,) + tile, src.dtype),
            pltpu.VMEM((BLOCK,) + tile, src.dtype),
            pltpu.SemaphoreType.DMA((DEPTH,)),
            pltpu.SemaphoreType.DMA,
            pltpu.SemaphoreType.DMA((DEPTH,)),
        ],
        compiler_params=pltpu.CompilerParams(vmem_limit_bytes=VMEM_BYTES),
        cost_estimate=pl.CostEstimate(flops=10 ** 9, bytes_accessed=sum(p[2] for p in pieces) * 2048, transcendentals=0),
    )(scal, src, after)


def place_kernel(c0, size, has_prev, scal_ref, fresh_ref, own, near, far0, far1, *refs):
    out = refs[1] if has_prev else refs[0]
    buf, in_sem, out_sem = refs[-3:]
    me = scal_ref[4]
    new_slot = lax.rem(scal_ref[me], WINDOW)
    count = size // BLOCK

    def in_copies(i):
        slot = lax.rem(i, DEPTH)
        local = pl.ds(i * BLOCK, BLOCK)
        whole = pl.ds(c0 + i * BLOCK, BLOCK)
        views = (own.at[whole], near.at[whole], far0.at[local], far1.at[local])
        return [
            pltpu.make_async_copy(view, buf.at[slot, :, :, me ^ j], in_sem.at[slot, j])
            for j, view in enumerate(views)
        ]

    def out_copy(i):
        slot = lax.rem(i, DEPTH)
        return pltpu.make_async_copy(buf.at[slot], out.at[pl.ds(c0 + i * BLOCK, BLOCK)], out_sem.at[slot])

    for i in range(min(DEPTH - 1, count)):
        for copy in in_copies(i):
            copy.start()

    @pl.loop(0, count)
    def _(i):
        for copy in in_copies(i):
            copy.wait()
        spot = new_slot - (c0 + i * BLOCK)

        @pl.when((spot >= 0) & (spot < BLOCK))
        def _():
            buf[lax.rem(i, DEPTH), spot] = fresh_ref[...]

        out_copy(i).start()
        ahead = i + DEPTH - 1

        @pl.when(ahead < count)
        def _():
            @pl.when(i >= 1)
            def _():
                out_copy(i - 1).wait()

            for copy in in_copies(ahead):
                copy.start()

    for i in range(max(count - DEPTH, 0), count):
        out_copy(i).wait()


def place(scal, fresh, own, near, far0, far1, c0, prev):
    size = far0.shape[0]
    hbm = pl.BlockSpec(memory_space=pltpu.HBM)
    operands = [scal, fresh, own, near, far0, far1]
    if prev is not None:
        operands.append(prev)
    halves, pair, lanes = own.shape[1:]
    return pl.pallas_call(
        functools.partial(place_kernel, c0, size, prev is not None),
        out_shape=jax.ShapeDtypeStruct((WINDOW, halves, 4, pair, lanes), own.dtype),
        in_specs=[pl.BlockSpec(memory_space=pltpu.SMEM), pl.BlockSpec(memory_space=pltpu.VMEM)] + [hbm] * (len(operands) - 2),
        out_specs=hbm,
        scratch_shapes=[
            pltpu.VMEM((DEPTH, BLOCK, halves, 4, pair, lanes), own.dtype),
            pltpu.SemaphoreType.DMA((DEPTH, 4)),
            pltpu.SemaphoreType.DMA((DEPTH,)),
        ],
        input_output_aliases={} if prev is None else {6: 0},
        compiler_params=pltpu.CompilerParams(vmem_limit_bytes=VMEM_BYTES),
        cost_estimate=pl.CostEstimate(flops=10 ** 9, bytes_accessed=size * 8192, transcendentals=0),
    )(*operands)


def rotate(heads, positions):
    head_dim = heads.shape[-1]
    half_dim = head_dim // 2
    inv_freq = THETA ** (-2.0 * jnp.arange(half_dim, dtype=jnp.float32) / head_dim)
    angles = positions.astype(jnp.float32).reshape(positions.shape + (1,) * (heads.ndim - 1)) * inv_freq
    cos_part = jnp.cos(angles)
    sin_part = jnp.sin(angles)
    first_half = heads[..., :half_dim].astype(jnp.float32)
    second_half = heads[..., half_dim:].astype(jnp.float32)
    return jnp.concatenate([first_half * cos_part - second_half * sin_part, second_half * cos_part + first_half * sin_part], axis=-1).astype(jnp.bfloat16)


def normalize(residual, norm_gain):
    resid_f32 = residual.astype(jnp.float32)
    inv_rms = lax.rsqrt(jnp.mean(resid_f32 * resid_f32, axis=-1, keepdims=True) + EPS)
    return (resid_f32 * inv_rms * norm_gain.astype(jnp.float32)).astype(jnp.bfloat16)


def project(normed, weight):
    return jnp.dot(normed, weight, preferred_element_type=jnp.float32).astype(jnp.bfloat16)


def split_lanes(array):
    halves = array.shape[-1] // LANES
    return jnp.swapaxes(array.reshape(array.shape[:-1] + (halves, LANES)), -3, -2)


def attend_heads(q_heads, k_new, v_new, k_prefill, v_prefill, lengths):
    scale = q_heads.shape[-1] ** 0.5
    positions = jnp.arange(k_prefill.shape[1], dtype=jnp.int32)[None, :]
    live = (positions < lengths[:, None]) & (positions > lengths[:, None] - WINDOW)
    scores = jnp.einsum('rkgd,rwkd->rkgw', q_heads, k_prefill, preferred_element_type=jnp.float32) / scale
    scores = jnp.where(live[:, None, None, :], scores, -jnp.inf)
    new_score = jnp.sum(q_heads.astype(jnp.float32) * k_new.astype(jnp.float32)[:, :, None, :], axis=-1, keepdims=True) / scale
    top = jnp.maximum(jnp.max(scores, axis=-1, keepdims=True), new_score)
    exp_scores = jnp.exp(scores - top)
    new_exp = jnp.exp(new_score - top)
    total = jnp.sum(exp_scores, axis=-1, keepdims=True) + new_exp
    weights = (exp_scores / total).astype(jnp.bfloat16)
    new_weight = (new_exp / total).astype(jnp.bfloat16)
    mixed = jnp.einsum('rkgw,rwkd->rkgd', weights, v_prefill, preferred_element_type=jnp.float32)
    mixed = mixed + new_weight.astype(jnp.float32) * v_new.astype(jnp.float32)[:, :, None, :]
    return mixed.astype(jnp.bfloat16)


def solution(mesh):
    group = mesh.shape['sh']
    head_spec = P('dp', None, 'sh', None)
    row_spec = P(('dp', 'sh'))
    full_spec = P(None, None)

    def swap(array, j):
        return lax.ppermute(array, 'sh', [(i, i ^ j) for i in range(group)])

    def per_device(k_prefill, v_prefill, lengths, residual, norm_gain, w_query, w_key, w_value, w_out):
        kv_heads, head_dim = k_prefill.shape[2:]
        me = lax.axis_index('sh')
        by_row = jnp.arange(group, dtype=jnp.int32) ^ me
        scal = jnp.concatenate([lengths, me[None].astype(jnp.int32)])
        my_length = lax.dynamic_slice_in_dim(lengths, me, 1)

        all_resid = jnp.concatenate([residual] + [swap(residual, j) for j in range(1, group)], axis=0)
        all_resid = jnp.take(all_resid, by_row, axis=0)

        k_src, v_src = split_lanes(k_prefill), split_lanes(v_prefill)

        def far_pieces(chunks):
            starts = [sum(chunks[:i]) for i in range(len(chunks))]
            return [[(2, c0, size), (3, c0, size)] for c0, size in zip(starts, chunks)]

        def send(src, chunks, after):
            far = []
            for pieces in far_pieces(chunks):
                built = build(scal, src, pieces, after)
                far.append([swap(a, p[0]) for a, p in zip(built, pieces)])
                after = built[0]
            own, near = build(scal, src, [(0, 0, WINDOW), (1, 0, WINDOW)], after)
            return own, swap(near, 1), far

        k_own, k_near, k_far = send(k_src, K_CHUNKS, scal)

        normed = normalize(all_resid, norm_gain)
        kv_width = kv_heads * head_dim
        q_width = w_query.shape[1] // group
        q_heads = project(normed, lax.dynamic_slice_in_dim(w_query, me * q_width, q_width, axis=1))
        q_heads = rotate(q_heads.reshape(group, kv_heads, q_width // kv_width, head_dim), lengths)
        k_new = project(normed, lax.dynamic_slice_in_dim(w_key, me * kv_width, kv_width, axis=1))
        v_new = project(normed, lax.dynamic_slice_in_dim(w_value, me * kv_width, kv_width, axis=1))
        k_new = rotate(k_new.reshape(group, kv_heads, head_dim), lengths)
        v_new = v_new.reshape(group, kv_heads, head_dim)
        mixed = attend_heads(q_heads, k_new, v_new, k_prefill, v_prefill, lengths).reshape(group, q_width)
        mixed = jnp.take(mixed, by_row, axis=0)
        mine = [mixed[:1]] + [swap(mixed[j:j + 1], j) for j in range(1, group)]

        v_own, v_near, v_far = send(v_src, V_CHUNKS, mixed)

        attn_out = jnp.take(jnp.concatenate(mine, axis=0), by_row, axis=0).reshape(1, group * q_width)
        resid_out = (residual.astype(jnp.float32) + jnp.dot(attn_out, w_out, preferred_element_type=jnp.float32)).astype(jnp.bfloat16)

        own_normed = normalize(residual, norm_gain)
        k_fresh = rotate(project(own_normed, w_key).reshape(1, group * kv_heads, head_dim), my_length)
        v_fresh = project(own_normed, w_value).reshape(1, group * kv_heads, head_dim)

        def cache(fresh, own, near, far):
            fresh = split_lanes(fresh[0])
            fresh = fresh.reshape(fresh.shape[0], group, kv_heads, LANES)
            out, c0 = None, 0
            for far0, far1 in far:
                out = place(scal, fresh, own, near, far0, far1, c0, out)
                c0 += far0.shape[0]
            return jnp.transpose(out, (0, 2, 3, 1, 4)).reshape(1, WINDOW, group * kv_heads, head_dim)

        return resid_out, cache(k_fresh, k_own, k_near, k_far), cache(v_fresh, v_own, v_near, v_far)

    return jax.shard_map(per_device, mesh=mesh, in_specs=(head_spec, head_spec, P('dp'), P(('dp', 'sh'), None), P(None), full_spec, full_spec, full_spec, full_spec), out_specs=(P(('dp', 'sh'), None), row_spec, row_spec), check_vma=False)
```

time: 839 us -> 432 us (0.51)
  blocking collectives: 335 us -> 0 us
  local copies, waits for them, and re-layouts: 133 us -> 5.41 us
  Pallas kernels: 0 us -> 108 us
  other arithmetic: 76.7 us -> 12.5 us
  matrix products: 58.2 us -> 68.1 us
    all_to_all x1 -> x0, blocking collectives: 335 us -> none  [per_device(): k_rows = lax.all_to_all(k_prefill, 'sh', 0, 2, tiled=True)]
    all_to_all x1 -> x0, waiting for transfers between devices: 219 us -> none  [per_device(): v_rows = lax.all_to_all(v_prefill, 'sh', 0, 2, tiled=True)]
    ppermute x0 -> x20, waiting for transfers between devices: none -> 216 us  [swap(): return lax.ppermute(array, 'sh', [(i, i ^ j) for i in range(group)])]
    all_to_all x4 -> x0, local copies, waits for them, and re-layouts: 133 us -> none  [the longest x2 66.4 us: per_device(): k_rows = lax.all_to_all(k_prefill, 'sh', 0, 2, tiled=True)]
    pallas_call x0 -> x14, Pallas kernels: none -> 108 us  [the longest x8 73.8 us: build(): pl.pallas_call(functools.partial(build_kernel, pieces), out_shape=[jax.Sh...]
    select_n x3, other arithmetic: 74.9 us -> 0.09 us  [the longest x1 0.08 us: per_device(): mixed = jnp.take(mixed, by_row, axis=0)]
    ppermute x0 -> x20, starting transfers between devices: none -> 15.7 us  [swap(): return lax.ppermute(array, 'sh', [(i, i ^ j) for i in range(group)])]
    dot_general x6 -> x8, matrix products: 58.2 us -> 68.1 us  [the longest x5 23.9 us: project(): jnp.dot(normed, weight, preferred_element_type=jnp.float32)]
  transfers between devices with their start and end apart: 1 -> 20, of which waited for: 1 -> 9; matrix products, arithmetic and copies ran while one was open for 6% -> 20% of each run, Pallas kernels for 0% -> 24%
where the time goes in v1:
time: 432 us; the launch traced here: 428 us
  waiting for transfers between devices  216 us (50%)
  Pallas kernels  108 us (25%)
  matrix products  68.1 us (16%)
  starting transfers between devices  15.7 us (4%)
  other arithmetic  12.5 us (3%)
  local copies, waits for them, and re-layouts  5.41 us (1%)
    ppermute x20, waiting for transfers between devices, swap(): return lax.ppermute(array, 'sh', [(i, i ^ j) for i in range(group)])  216 us
    pallas_call x8, Pallas kernels, build(): pl.pallas_call(functools.partial(build_kernel, pieces), out_shape=[jax.Sh...  73.8 us
    pallas_call x6, Pallas kernels, place(): pl.pallas_call(functools.partial(place_kernel, c0, size, prev is not None...  34.4 us
    dot_general x5, matrix products, project(): jnp.dot(normed, weight, preferred_element_type=jnp.float32)  23.9 us
    dot_general x1, matrix products, attend_heads(): jnp.einsum('rkgd,rwkd->rkgw', q_heads, k_prefill, preferred_element_type=...  18.7 us
    ppermute x20, starting transfers between devices, swap(): return lax.ppermute(array, 'sh', [(i, i ^ j) for i in range(group)])  15.7 us
    dot_general x1, matrix products, attend_heads(): jnp.einsum('rkgw,rwkd->rkgd', weights, v_prefill, preferred_element_type=...  13.5 us
    dot_general x1, matrix products, per_device(): jnp.dot(attn_out, w_out, preferred_element_type=jnp.float32)  12 us
  transfers between devices with their start and end apart: 20, of which 9 were waited for; matrix products, arithmetic and copies ran while one was open for 20% of the time, Pallas kernels for 24%

profile of v1, /device:TPU:0, one launch (start us, length us, event | category | flops | bytes accessed | tf_op | source)
XLA Modules:
  0.0 428.4 jit_solution(6380017676224603498)
XLA Ops:
  0.6 2.7 collective-permute-start.2
  5.3 4.3 shard_map.112
  9.6 8.8 %shard_map.113 = (bf16[1536,2,2,128]{3,2,1,0:T(2,128)(2,1)}, bf16[1536,2,2,128]{3,2,1,0:T(2,128)(2,1)}) custom-call(s32[5]{0:T(128)} %pad_add_fusion.scal_ref._, bf16[4,7168,2,2,128]{4,3,2,1,0:T(2,128)(2,1)} %bitcast.42, bf16[512,2,2,128]{3,2,1,0:T(2,128)(2,1)} %get-tuple-element.20._), custom_call_target="tpu_custom_call" | custom-call | flops 1000000000 | bytes 6291456 | tf_op jit(solution)/shard_map/pallas_call | solution.py:104
  18.7 7.9 %shard_map.114 = (bf16[2048,2,2,128]{3,2,1,0:T(2,128)(2,1)}, bf16[2048,2,2,128]{3,2,1,0:T(2,128)(2,1)}) custom-call(s32[5]{0:T(128)} %pad_add_fusion.scal_ref._, bf16[4,7168,2,2,128]{4,3,2,1,0:T(2,128)(2,1)} %bitcast.43, bf16[1536,2,2,128]{3,2,1,0:T(2,128)(2,1)} %get-tuple-element.21._), custom_call_target="tpu_custom_call" | custom-call | flops 1000000000 | bytes 8388608 | tf_op jit(solution)/shard_map/pallas_call | solution.py:104
  32.9 16.3 %shard_map.115 = (bf16[4096,2,2,128]{3,2,1,0:T(2,128)(2,1)}, bf16[4096,2,2,128]{3,2,1,0:T(2,128)(2,1)}) custom-call(s32[5]{0:T(128)} %pad_add_fusion.scal_ref._, bf16[4,7168,2,2,128]{4,3,2,1,0:T(2,128)(2,1)} %bitcast.44, bf16[2048,2,2,128]{3,2,1,0:T(2,128)(2,1)} %get-tuple-element.22._), custom_call_target="tpu_custom_call" | custom-call | flops 1000000000 | bytes 16777216 | tf_op jit(solution)/shard_map/pallas_call | solution.py:104
  53.4 4.2 fusion.23
  57.6 2.7 fusion.26
  61.7 18.7 %fusion.71 = (f32[4,2,2]{2,1,0:T(2,128)S(1)}, f32[4,2,2,7168]{3,2,1,0:T(2,128)S(1)}) fusion(bf16[4,7168,2,256]{3,2,1,0:T(2,128)(2,1)} %param.11, bf16[4,2,2,128]{3,2,1,0:T(2,128)(2,1)S(1)} %get-tuple-element.39, bf16[4,2,2,128]{3,2,1,0:T(2,128)(2,1)S(1)} %get-tuple-element.38, pred[4,7168]{1,0:T(4,128)(4,1)} %fusion.38), kind=kOutput, calls=%fused_computation.101 | convolution fusion | flops 59080688 | bytes 29855808 | tf_op jit(solution)/shard_map/rkgd,rwkd->rkgw/dot_general | solution.py:227
  81.1 2.7 fusion.32
  83.8 13.5 %fusion.20 = bf16[4,2,2,256]{3,2,1,0:T(2,128)(2,1)S(1)} fusion(bf16[4,7168,2,256]{3,2,1,0:T(2,128)(2,1)} %param.12, f32[4,2,2,7168]{3,2,1,0:T(2,128)S(1)} %get-tuple-element.53, f32[4,2,2]{2,1,0:T(2,128)S(1)} %get-tuple-element.37, f32[4,2,2]{2,1,0:T(2,128)S(1)} %multiply_maximum_fusion, f32[4,2,256]{2,1,0:T(2,128)S(1)} %reshape.348, ...), kind=kOutput, calls=%fused_computation.18 | convolution fusion | flops 59076608 | bytes 29835456 | tf_op jit(solution)/shard_map/rkgw,rwkd->rkgd/dot_general | solution.py:236
  99.4 34.2 %collective-permute-done.5 = bf16[1,1024]{1,0:T(2,128)(2,1)S(1)} collective-permute-done((bf16[1,1024]{1,0:T(2,128)(2,1)S(1)}, bf16[1,1024]{1,0:T(2,128)(2,1)S(1)}, u32[]{:S(2)}, u32[]{:S(2)}) %collective-permute-start.5) | collective-permute-done | bytes 2080 | tf_op jit(solution)/shard_map/ppermute | solution.py:248
  133.9 3.3 collective-permute-done.4
  138.9 13.7 %collective-permute-done.11.far0 = bf16[512,2,2,128]{3,2,1,0:T(2,128)(2,1)S(1)} collective-permute-done((bf16[512,2,2,128]{3,2,1,0:T(2,128)(2,1)S(1)}, bf16[512,2,2,128]{3,2,1,0:T(2,128)(2,1)S(1)}, u32[]{:S(2)}, u32[]{:S(2)}) %collective-permute-start.11) | collective-permute-done | bytes 524320 | tf_op jit(solution)/shard_map/ppermute | solution.py:248
  154.5 10.6 %shard_map.119 = (bf16[2048,2,2,128]{3,2,1,0:T(2,128)(2,1)}, bf16[2048,2,2,128]{3,2,1,0:T(2,128)(2,1)}) custom-call(s32[5]{0:T(128)} %pad_add_fusion.scal_ref._, bf16[4,7168,2,2,128]{4,3,2,1,0:T(2,128)(2,1)} %bitcast.45, bf16[4,1024]{1,0:T(4,128)(2,1)} %copy-done.7), custom_call_target="tpu_custom_call" | custom-call | flops 1000000000 | bytes 8388608 | tf_op jit(solution)/shard_map/pallas_call | solution.py:104
  165.2 6.1 %shard_map.120 = (bf16[1536,2,2,128]{3,2,1,0:T(2,128)(2,1)}, bf16[1536,2,2,128]{3,2,1,0:T(2,128)(2,1)}) custom-call(s32[5]{0:T(128)} %pad_add_fusion.scal_ref._, bf16[4,7168,2,2,128]{4,3,2,1,0:T(2,128)(2,1)} %bitcast.46, bf16[2048,2,2,128]{3,2,1,0:T(2,128)(2,1)} %get-tuple-element.28._), custom_call_target="tpu_custom_call" | custom-call | flops 1000000000 | bytes 6291456 | tf_op jit(solution)/shard_map/pallas_call | solution.py:104
  171.3 3.4 shard_map.121
  174.7 16.4 %shard_map.122 = (bf16[4096,2,2,128]{3,2,1,0:T(2,128)(2,1)}, bf16[4096,2,2,128]{3,2,1,0:T(2,128)(2,1)}) custom-call(s32[5]{0:T(128)} %pad_add_fusion.scal_ref._, bf16[4,7168,2,2,128]{4,3,2,1,0:T(2,128)(2,1)} %bitcast.48, bf16[512,2,2,128]{3,2,1,0:T(2,128)(2,1)} %get-tuple-element.30._), custom_call_target="tpu_custom_call" | custom-call | flops 1000000000 | bytes 16777216 | tf_op jit(solution)/shard_map/pallas_call | solution.py:104
  193.1 2.0 collective-permute-start.19
  195.1 7.2 %fusion.44 = f32[1,2048]{1,0:T(1,128)S(1)} fusion(bf16[3584,2048]{1,0:T(8,128)(2,1)} %param.17, f32[3584]{0:T(1024)} %copy-done.1, bf16[1,3584]{1,0:T(2,128)(2,1)} %param.14, f32[]{:T(128)S(6)} %rsqrt.13), kind=kOutput, calls=%fused_computation.41 | convolution fusion | flops 14694400 | bytes 14709764 | tf_op jit(solution)/shard_map/dot_general | solution.py:215
  203.6 7.2 %fusion.42 = f32[1,2048]{1,0:T(1,128)S(1)} fusion(bf16[3584,2048]{1,0:T(8,128)(2,1)} %param.18, f32[3584]{0:T(1024)S(1)} %copy-done.2, bf16[1,3584]{1,0:T(2,128)(2,1)S(1)} %copy-done.6, f32[]{:T(128)S(6)} %rsqrt.13), kind=kOutput, calls=%fused_computation.39 | convolution fusion | flops 14694400 | bytes 14709764 | tf_op jit(solution)/shard_map/dot_general | solution.py:215
  213.5 25.7 %collective-permute-done.8.far1 = bf16[2048,2,2,128]{3,2,1,0:T(2,128)(2,1)S(1)} collective-permute-done((bf16[2048,2,2,128]{3,2,1,0:T(2,128)(2,1)}, bf16[2048,2,2,128]{3,2,1,0:T(2,128)(2,1)S(1)}, u32[]{:S(2)}, u32[]{:S(2)}) %collective-permute-start.8) | collective-permute-done | bytes 2097184 | tf_op jit(solution)/shard_map/ppermute | solution.py:248
  239.4 45.4 %collective-permute-done.18.far0 = bf16[2048,2,2,128]{3,2,1,0:T(2,128)(2,1)} collective-permute-done((bf16[2048,2,2,128]{3,2,1,0:T(2,128)(2,1)}, bf16[2048,2,2,128]{3,2,1,0:T(2,128)(2,1)}, u32[]{:S(2)}, u32[]{:S(2)}) %collective-permute-start.18) | collective-permute-done | bytes 2097184 | tf_op jit(solution)/shard_map/ppermute | solution.py:248
  286.7 42.5 %collective-permute-done.19.far1 = bf16[2048,2,2,128]{3,2,1,0:T(2,128)(2,1)} collective-permute-done((bf16[2048,2,2,128]{3,2,1,0:T(2,128)(2,1)}, bf16[2048,2,2,128]{3,2,1,0:T(2,128)(2,1)}, u32[]{:S(2)}, u32[]{:S(2)}) %collective-permute-start.19) | collective-permute-done | bytes 2097184 | tf_op jit(solution)/shard_map/ppermute | solution.py:248
  331.1 12.0 %fusion.12 = bf16[1,3584]{1,0:T(2,128)(2,1)} fusion(bf16[4096,1]{0,1:T(2,128)(2,1)S(1)} %bitcast.51, bf16[4096,3584]{1,0:T(8,128)(2,1)} %param.19, bf16[1,3584]{1,0:T(2,128)(2,1)S(1)} %copy-done.6), kind=kOutput, calls=%fused_computation.12 | convolution fusion | flops 29370880 | bytes 29382656 | tf_op jit(solution)/shard_map/dot_general | solution.py:293
  343.0 3.4 shard_map.116.refs_0_
  346.4 6.1 %shard_map.117.refs_0_ = bf16[4096,2,4,2,128]{4,3,2,1,0:T(2,128)(2,1)} custom-call(s32[5]{0:T(128)} %pad_add_fusion.scal_ref._, bf16[2,4,2,128]{3,2,1,0:T(2,128)(2,1)} %bitcast.56, bf16[4096,2,2,128]{3,2,1,0:T(2,128)(2,1)} %get-tuple-element.23.own, bf16[4096,2,2,128]{3,2,1,0:T(2,128)(2,1)} %collective-permute-done.6.near, ...), custom_call_target="tpu_custom_call", output_to_operand_aliasing={{}: (6, {})} | custom-call | flops 1000000000 | bytes 12582912 | tf_op jit(solution)/shard_map/pallas_call | solution.py:180
  352.5 7.8 %shard_map.118 = bf16[4096,2,4,2,128]{4,3,2,1,0:T(2,128)(2,1)} custom-call(s32[5]{0:T(128)} %pad_add_fusion.scal_ref._, bf16[2,4,2,128]{3,2,1,0:T(2,128)(2,1)} %bitcast.57, bf16[4096,2,2,128]{3,2,1,0:T(2,128)(2,1)} %get-tuple-element.23.own, bf16[4096,2,2,128]{3,2,1,0:T(2,128)(2,1)} %collective-permute-done.6.near, ...), custom_call_target="tpu_custom_call", output_to_operand_aliasing={{}: (6, {})} | custom-call | flops 1000000000 | bytes 16777216 | tf_op jit(solution)/shard_map/pallas_call | solution.py:180
  360.3 7.8 %shard_map.123.refs_0_ = bf16[4096,2,4,2,128]{4,3,2,1,0:T(2,128)(2,1)} custom-call(s32[5]{0:T(128)} %pad_add_fusion.scal_ref._, bf16[2,4,2,128]{3,2,1,0:T(2,128)(2,1)} %bitcast.52, bf16[4096,2,2,128]{3,2,1,0:T(2,128)(2,1)} %get-tuple-element.31.own, bf16[4096,2,2,128]{3,2,1,0:T(2,128)(2,1)} %collective-permute-done.13.near, ...), custom_call_target="tpu_custom_call" | custom-call | flops 1000000000 | bytes 16777216 | tf_op jit(solution)/shard_map/pallas_call | solution.py:180
  368.1 6.6 %collective-permute-done.16.far0 = bf16[1536,2,2,128]{3,2,1,0:T(2,128)(2,1)} collective-permute-done((bf16[1536,2,2,128]{3,2,1,0:T(2,128)(2,1)}, bf16[1536,2,2,128]{3,2,1,0:T(2,128)(2,1)}, u32[]{:S(2)}, u32[]{:S(2)}) %collective-permute-start.16) | collective-permute-done | bytes 1572896 | tf_op jit(solution)/shard_map/ppermute | solution.py:248
  374.7 44.1 %collective-permute-done.17.far1 = bf16[1536,2,2,128]{3,2,1,0:T(2,128)(2,1)} collective-permute-done((bf16[1536,2,2,128]{3,2,1,0:T(2,128)(2,1)}, bf16[1536,2,2,128]{3,2,1,0:T(2,128)(2,1)}, u32[]{:S(2)}, u32[]{:S(2)}) %collective-permute-start.17) | collective-permute-done | bytes 1572896 | tf_op jit(solution)/shard_map/ppermute | solution.py:248
  418.7 6.1 %shard_map.124.refs_0_ = bf16[4096,2,4,2,128]{4,3,2,1,0:T(2,128)(2,1)} custom-call(s32[5]{0:T(128)} %pad_add_fusion.scal_ref._, bf16[2,4,2,128]{3,2,1,0:T(2,128)(2,1)} %bitcast.53, bf16[4096,2,2,128]{3,2,1,0:T(2,128)(2,1)} %get-tuple-element.31.own, bf16[4096,2,2,128]{3,2,1,0:T(2,128)(2,1)} %collective-permute-done.13.near, ...), custom_call_target="tpu_custom_call", output_to_operand_aliasing={{}: (6, {})} | custom-call | flops 1000000000 | bytes 12582912 | tf_op jit(solution)/shard_map/pallas_call | solution.py:180
  424.8 3.4 shard_map.125
  (104 shorter events, 29.7 us)
Async XLA Ops:
  0.6 49.3 %collective-permute-start.2 = (bf16[1,3584]{1,0:T(2,128)(2,1)}, bf16[1,3584]{1,0:T(2,128)(2,1)}, u32[]{:S(2)}, u32[]{:S(2)}) collective-permute-start(bf16[1,3584]{1,0:T(2,128)(2,1)} %param.14), channel_id=1, source_target_pairs={{0,3},{1,2},{2,1},{3,0},{4,7},{5,6},{6,5},{7,4},{8,11},{9,10},{10,... | collective-permute-start | bytes 21512 | tf_op jit(solution)/shard_map/ppermute | solution.py:248
  3.3 46.6 %collective-permute-start.1 = (bf16[1,3584]{1,0:T(2,128)(2,1)}, bf16[1,3584]{1,0:T(2,128)(2,1)}, u32[]{:S(2)}, u32[]{:S(2)}) collective-permute-start(bf16[1,3584]{1,0:T(2,128)(2,1)} %param.14), channel_id=1, source_target_pairs={{0,2},{1,3},{2,0},{3,1},{4,6},{5,7},{6,4},{7,5},{8,10},{9,11},{10,... | collective-permute-start | bytes 21512 | tf_op jit(solution)/shard_map/ppermute | solution.py:248
  3.9 47.1 %collective-permute-start = (bf16[1,3584]{1,0:T(2,128)(2,1)}, bf16[1,3584]{1,0:T(2,128)(2,1)}, u32[]{:S(2)}, u32[]{:S(2)}) collective-permute-start(bf16[1,3584]{1,0:T(2,128)(2,1)} %param.14), channel_id=1, source_target_pairs={{0,1},{1,0},{2,3},{3,2},{4,5},{5,4},{6,7},{7,6},{8,9},{9,8},{10,11... | collective-permute-start | bytes 21512 | tf_op jit(solution)/shard_map/ppermute | solution.py:248
  18.4 174.5 %collective-permute-start.9 = (bf16[1536,2,2,128]{3,2,1,0:T(2,128)(2,1)}, bf16[1536,2,2,128]{3,2,1,0:T(2,128)(2,1)}, u32[]{:S(2)}, u32[]{:S(2)}) collective-permute-start(bf16[1536,2,2,128]{3,2,1,0:T(2,128)(2,1)} %get-tuple-element.21._), channel_id=1, source_target_pairs={{0,2},{1,3},{2,0},{3,1},{4,6},{5,7},{6,4},{7,5},{8,10},{9,11},{10,... | collective-permute-start | bytes 4718600 | tf_op jit(solution)/shard_map/ppermute | solution.py:248
  26.6 166.5 %collective-permute-start.7 = (bf16[2048,2,2,128]{3,2,1,0:T(2,128)(2,1)}, bf16[2048,2,2,128]{3,2,1,0:T(2,128)(2,1)}, u32[]{:S(2)}, u32[]{:S(2)}) collective-permute-start(bf16[2048,2,2,128]{3,2,1,0:T(2,128)(2,1)} %get-tuple-element.22._), channel_id=1, source_target_pairs={{0,2},{1,3},{2,0},{3,1},{4,6},{5,7},{6,4},{7,5},{8,10},{9,11},{10,... | collective-permute-start | bytes 6291464 | tf_op jit(solution)/shard_map/ppermute | solution.py:248
  49.9 31.2 %copy-start.1 = (f32[3584]{0:T(1024)}, f32[3584]{0:T(1024)S(1)}, u32[]{:S(2)}) copy-start(f32[3584]{0:T(1024)S(1)} %convert_element_type.119) | copy-start | bytes 43012
  49.9 281.1 %collective-permute-start.6 = (bf16[4096,2,2,128]{3,2,1,0:T(2,128)(2,1)}, bf16[4096,2,2,128]{3,2,1,0:T(2,128)(2,1)}, u32[]{:S(2)}, u32[]{:S(2)}) collective-permute-start(bf16[4096,2,2,128]{3,2,1,0:T(2,128)(2,1)} %get-tuple-element.24), channel_id=1, source_target_pairs={{0,1},{1,0},{2,3},{3,2},{4,5},{5,4},{6,7},{7,6},{8,9},{9,8},{10,11... | collective-permute-start | bytes 12582920 | tf_op jit(solution)/shard_map/ppermute | solution.py:248
  49.9 143.1 %collective-permute-start.10 = (bf16[1536,2,2,128]{3,2,1,0:T(2,128)(2,1)}, bf16[1536,2,2,128]{3,2,1,0:T(2,128)(2,1)}, u32[]{:S(2)}, u32[]{:S(2)}) collective-permute-start(bf16[1536,2,2,128]{3,2,1,0:T(2,128)(2,1)} %get-tuple-element.26), channel_id=1, source_target_pairs={{0,3},{1,2},{2,1},{3,0},{4,7},{5,6},{6,5},{7,4},{8,11},{9,10},{10,... | collective-permute-start | bytes 4718600 | tf_op jit(solution)/shard_map/ppermute | solution.py:248
  61.7 19.4 %copy-start.8 = (pred[4]{0:T(512)(128)(4,1)S(1)}, pred[4]{0:T(512)(128)(4,1)}, u32[]{:S(2)}) copy-start(pred[4]{0:T(512)(128)(4,1)} %compare_and_fusion) | copy-start | bytes 16
  83.8 54.8 %copy-start.3 = (bf16[512,2,2,128]{3,2,1,0:T(2,128)(2,1)S(1)}, bf16[512,2,2,128]{3,2,1,0:T(2,128)(2,1)}, u32[]{:S(2)}) copy-start(bf16[512,2,2,128]{3,2,1,0:T(2,128)(2,1)} %get-tuple-element.20._) | copy-start | bytes 1572868
  83.8 69.6 %copy-start.5 = (bf16[1,3584]{1,0:T(2,128)(2,1)S(1)}, bf16[1,3584]{1,0:T(2,128)(2,1)}, u32[]{:S(2)}) copy-start(bf16[1,3584]{1,0:T(2,128)(2,1)} %param.14) | copy-start | bytes 21508
  98.0 55.3 %copy-start.7 = (bf16[4,1024]{1,0:T(4,128)(2,1)}, bf16[4,1024]{1,0:T(4,128)(2,1)S(1)}, u32[]{:S(2)}) copy-start(bf16[4,1024]{1,0:T(4,128)(2,1)S(1)} %broadcast_select_fusion.1._) | copy-start | bytes 24580
  98.7 35.0 %collective-permute-start.5 = (bf16[1,1024]{1,0:T(2,128)(2,1)S(1)}, bf16[1,1024]{1,0:T(2,128)(2,1)S(1)}, u32[]{:S(2)}, u32[]{:S(2)}) collective-permute-start(bf16[1,1024]{1,0:T(2,128)(2,1)S(1)} %get-tuple-element.41), channel_id=1, source_target_pairs={{0,3},{1,2},{2,1},{3,0},{4,7},{5,6},{6,5},{7,4},{8,11},{9,10},{10,... | collective-permute-start | bytes 6152 | tf_op jit(solution)/shard_map/ppermute | solution.py:248
  133.6 3.6 collective-permute-start.4
  137.2 1.3 collective-permute-start.3
  138.5 14.0 %collective-permute-start.11 = (bf16[512,2,2,128]{3,2,1,0:T(2,128)(2,1)S(1)}, bf16[512,2,2,128]{3,2,1,0:T(2,128)(2,1)S(1)}, u32[]{:S(2)}, u32[]{:S(2)}) collective-permute-start(bf16[512,2,2,128]{3,2,1,0:T(2,128)(2,1)S(1)} %copy-done.3), channel_id=1, source_target_pairs={{0,2},{1,3},{2,0},{3,1},{4,6},{5,7},{6,4},{7,5},{8,10},{9,11},{10,... | collective-permute-start | bytes 1572872 | tf_op jit(solution)/shard_map/ppermute | solution.py:248
  153.3 37.8 %collective-permute-start.12 = (bf16[512,2,2,128]{3,2,1,0:T(2,128)(2,1)}, bf16[512,2,2,128]{3,2,1,0:T(2,128)(2,1)}, u32[]{:S(2)}, u32[]{:S(2)}) collective-permute-start(bf16[512,2,2,128]{3,2,1,0:T(2,128)(2,1)} %get-tuple-element.27), channel_id=1, source_target_pairs={{0,3},{1,2},{2,1},{3,0},{4,7},{5,6},{6,5},{7,4},{8,11},{9,10},{10,... | collective-permute-start | bytes 1572872 | tf_op jit(solution)/shard_map/ppermute | solution.py:248
  191.1 11.2 %copy-start.15 = (s32[4]{0:T(128)S(1)}, s32[4]{0:T(128)}, u32[]{:S(2)}) copy-start(s32[4]{0:T(128)} %param.13) | copy-start | bytes 52
  191.1 12.5 %copy-start.2 = (f32[3584]{0:T(1024)S(1)}, f32[3584]{0:T(1024)}, u32[]{:S(2)}) copy-start(f32[3584]{0:T(1024)} %copy-done.1) | copy-start | bytes 43012
  191.1 12.5 %copy-start.6 = (bf16[1,3584]{1,0:T(2,128)(2,1)S(1)}, bf16[1,3584]{1,0:T(2,128)(2,1)}, u32[]{:S(2)}) copy-start(bf16[1,3584]{1,0:T(2,128)(2,1)} %param.14) | copy-start | bytes 21508
  191.1 48.1 %collective-permute-start.8 = (bf16[2048,2,2,128]{3,2,1,0:T(2,128)(2,1)}, bf16[2048,2,2,128]{3,2,1,0:T(2,128)(2,1)S(1)}, u32[]{:S(2)}, u32[]{:S(2)}) collective-permute-start(bf16[2048,2,2,128]{3,2,1,0:T(2,128)(2,1)} %get-tuple-element.25), channel_id=1, source_target_pairs={{0,3},{1,2},{2,1},{3,0},{4,7},{5,6},{6,5},{7,4},{8,11},{9,10},{10,... | collective-permute-start | bytes 6291464 | tf_op jit(solution)/shard_map/ppermute | solution.py:248
  192.9 91.9 %collective-permute-start.18 = (bf16[2048,2,2,128]{3,2,1,0:T(2,128)(2,1)}, bf16[2048,2,2,128]{3,2,1,0:T(2,128)(2,1)}, u32[]{:S(2)}, u32[]{:S(2)}) collective-permute-start(bf16[2048,2,2,128]{3,2,1,0:T(2,128)(2,1)} %get-tuple-element.28._), channel_id=1, source_target_pairs={{0,2},{1,3},{2,0},{3,1},{4,6},{5,7},{6,4},{7,5},{8,10},{9,11},{10,... | collective-permute-start | bytes 6291464 | tf_op jit(solution)/shard_map/ppermute | solution.py:248
  193.0 167.2 %collective-permute-start.13 = (bf16[4096,2,2,128]{3,2,1,0:T(2,128)(2,1)}, bf16[4096,2,2,128]{3,2,1,0:T(2,128)(2,1)}, u32[]{:S(2)}, u32[]{:S(2)}) collective-permute-start(bf16[4096,2,2,128]{3,2,1,0:T(2,128)(2,1)} %get-tuple-element.32), channel_id=1, source_target_pairs={{0,1},{1,0},{2,3},{3,2},{4,5},{5,4},{6,7},{7,6},{8,9},{9,8},{10,11... | collective-permute-start | bytes 12582920 | tf_op jit(solution)/shard_map/ppermute | solution.py:248
  193.1 136.0 %collective-permute-start.19 = (bf16[2048,2,2,128]{3,2,1,0:T(2,128)(2,1)}, bf16[2048,2,2,128]{3,2,1,0:T(2,128)(2,1)}, u32[]{:S(2)}, u32[]{:S(2)}) collective-permute-start(bf16[2048,2,2,128]{3,2,1,0:T(2,128)(2,1)} %get-tuple-element.35), channel_id=1, source_target_pairs={{0,3},{1,2},{2,1},{3,0},{4,7},{5,6},{6,5},{7,4},{8,11},{9,10},{10,... | collective-permute-start | bytes 6291464 | tf_op jit(solution)/shard_map/ppermute | solution.py:248
  202.3 9.8 %copy-start.12 = (bf16[1,1024]{1,0:T(2,128)(2,1)S(1)}, bf16[1,1024]{1,0:T(2,128)(2,1)}, u32[]{:S(2)}) copy-start(bf16[1,1024]{1,0:T(2,128)(2,1)} %copy-done.11) | copy-start | bytes 6148
  202.3 9.8 %copy-start.14 = (bf16[1,1024]{1,0:T(2,128)(2,1)S(1)}, bf16[1,1024]{1,0:T(2,128)(2,1)}, u32[]{:S(2)}) copy-start(bf16[1,1024]{1,0:T(2,128)(2,1)} %copy-done.13) | copy-start | bytes 6148
  202.3 11.2 %copy-start.9 = (pred[4]{0:T(512)(128)(4,1)S(1)}, pred[4]{0:T(512)(128)(4,1)}, u32[]{:S(2)}) copy-start(pred[4]{0:T(512)(128)(4,1)} %compare_and_fusion) | copy-start | bytes 16
  239.2 103.8 %copy-start = (bf16[2048,2,2,128]{3,2,1,0:T(2,128)(2,1)}, bf16[2048,2,2,128]{3,2,1,0:T(2,128)(2,1)S(1)}, u32[]{:S(2)}) copy-start(bf16[2048,2,2,128]{3,2,1,0:T(2,128)(2,1)S(1)} %collective-permute-done.8.far1) | copy-start | bytes 6291460
  239.2 185.6 %collective-permute-start.14 = (bf16[512,2,2,128]{3,2,1,0:T(2,128)(2,1)}, bf16[512,2,2,128]{3,2,1,0:T(2,128)(2,1)}, u32[]{:S(2)}, u32[]{:S(2)}) collective-permute-start(bf16[512,2,2,128]{3,2,1,0:T(2,128)(2,1)} %get-tuple-element.30._), channel_id=1, source_target_pairs={{0,2},{1,3},{2,0},{3,1},{4,6},{5,7},{6,4},{7,5},{8,10},{9,11},{10,... | collective-permute-start | bytes 1572872 | tf_op jit(solution)/shard_map/ppermute | solution.py:248
  284.8 89.9 %collective-permute-start.16 = (bf16[1536,2,2,128]{3,2,1,0:T(2,128)(2,1)}, bf16[1536,2,2,128]{3,2,1,0:T(2,128)(2,1)}, u32[]{:S(2)}, u32[]{:S(2)}) collective-permute-start(bf16[1536,2,2,128]{3,2,1,0:T(2,128)(2,1)} %get-tuple-element.29._), channel_id=1, source_target_pairs={{0,2},{1,3},{2,0},{3,1},{4,6},{5,7},{6,4},{7,5},{8,10},{9,11},{10,... | collective-permute-start | bytes 4718600 | tf_op jit(solution)/shard_map/ppermute | solution.py:248
  329.1 95.7 %collective-permute-start.15 = (bf16[512,2,2,128]{3,2,1,0:T(2,128)(2,1)}, bf16[512,2,2,128]{3,2,1,0:T(2,128)(2,1)}, u32[]{:S(2)}, u32[]{:S(2)}) collective-permute-start(bf16[512,2,2,128]{3,2,1,0:T(2,128)(2,1)} %get-tuple-element.33), channel_id=1, source_target_pairs={{0,3},{1,2},{2,1},{3,0},{4,7},{5,6},{6,5},{7,4},{8,11},{9,10},{10,... | collective-permute-start | bytes 1572872 | tf_op jit(solution)/shard_map/ppermute | solution.py:248
  331.0 87.7 %collective-permute-start.17 = (bf16[1536,2,2,128]{3,2,1,0:T(2,128)(2,1)}, bf16[1536,2,2,128]{3,2,1,0:T(2,128)(2,1)}, u32[]{:S(2)}, u32[]{:S(2)}) collective-permute-start(bf16[1536,2,2,128]{3,2,1,0:T(2,128)(2,1)} %get-tuple-element.34), channel_id=1, source_target_pairs={{0,3},{1,2},{2,1},{3,0},{4,7},{5,6},{6,5},{7,4},{8,11},{9,10},{10,... | collective-permute-start | bytes 4718600 | tf_op jit(solution)/shard_map/ppermute | solution.py:248
  (4 other events, 14.8 us)
